TPU v7x, 256 devices: a 8x8x2 block of a 8x8x16 slice. The times are simulated.
256 devices in a mesh: groups: 2 (over z), seq: 16 (over y, core), head: 8 (over x).
Axes of the slice: x: 8, y: 8, z: 2, core: 2. Of those that a mesh axis runs over, the one named last changes fastest.
The devices are a block of a 8x8x16 slice.
Arguments:
- queries: bfloat16 [4096, 8192], P(('groups', 'seq'), 'head'), parts along dimension 0
- new_keys: bfloat16 [4096, 1024], P(('groups', 'seq'), 'head'), parts along dimension 0, may hold values from -6 to 6
- new_values: bfloat16 [4096, 1024], P(('groups', 'seq'), 'head'), parts along dimension 0, may hold values from -6 to 6
- cache_keys: bfloat16 [32768, 1024], P(('groups', 'seq'), 'head'), parts along dimension 0
- cache_values: bfloat16 [32768, 1024], P(('groups', 'seq'), 'head'), parts along dimension 0, may hold values from -6 to 6
- valid_len: int32 [32], P('groups'), parts along dimension 0, may hold values from 1 to 1024, as said below
- block_of: int32 [32], P('groups'), parts along dimension 0, may hold values from 0 to 15, each once
Outputs:
- attended: bfloat16 [4096, 8192], P(('groups', 'seq'), 'head'), parts along dimension 0
There are 2 independent parts, one for each index of `groups`. A program takes and returns all parts, laid end to end along the dimension named above; each array names one. Nothing has to cross between parts.
Inputs may be any that keep to these rules, and one draw needn't show every extreme that they name: `valid_len`: some shard is full (1024 filled slots) in every draw; slot 0 of every shard is filled. `block_of`: A permutation of the 16 span blocks.
All inputs are finite; a program needn't handle non-finite values.
Results may differ from a plain program's by a relative error of at most 0.0027.
Values may be sent and summed in bfloat16 or wider, within the bound.
A program may use at most 192 MiB of HBM per device.

v0:
```python
import jax
import jax.numpy as jnp
from jax import lax
from jax.sharding import PartitionSpec as P

DH = 128
GROUP = 8


NEGATIVE = -1e30


def in_order(tiles, dim):
    shape = list(tiles.shape[1:])
    shape[dim] *= tiles.shape[0]
    return jnp.moveaxis(tiles, 0, dim).reshape(shape)


def from_everyone(array, axis):
    size = lax.axis_size(axis)
    return lax.all_to_all(
        jnp.broadcast_to(array[None], (size, *array.shape)), axis, 0, 0, tiled=True
    )


def gather_directly(array, axis, dim):
    return in_order(from_everyone(array, axis), dim)


def sent_together(arrays, axis, dim, along):
    both = jnp.concatenate(arrays, axis=along)
    filled, at, done = (gather_directly(both, axis, dim), 0, [])
    for a in arrays:
        done.append(lax.slice_in_dim(filled, at, at + a.shape[along], axis=along))
        at += a.shape[along]
    return tuple(done)


def lookup(table, where_at):
    picked = where_at[:, None] == jnp.arange(table.shape[0], dtype=jnp.int32)[None, :]
    return jnp.sum(jnp.where(picked, table[None, :], 0), axis=1)


def scores_of(query_rows, key_rows):
    heads = key_rows.shape[1] // DH
    query_four = query_rows.reshape(query_rows.shape[0], heads, GROUP, DH)
    key_three = key_rows.reshape(key_rows.shape[0], heads, DH)
    product = jnp.einsum(
        "rkgd,nkd->rkgn", query_four, key_three, preferred_element_type=jnp.float32
    )
    return product * DH ** (-0.5)


def visible(query_pos, key_pos, key_live):
    return (key_live[None, :] & (key_pos[None, :] <= query_pos[:, None]))[:, None, None, :]


def masked_max(scores, seen):
    return jnp.max(jnp.where(seen, scores, NEGATIVE), axis=-1)


def weights_of(scores, seen, top):
    return jnp.where(seen, jnp.exp(scores - top[..., None]), 0.0)


def accumulate(weights, value_rows):
    heads = value_rows.shape[1] // DH
    value_three = value_rows.reshape(value_rows.shape[0], heads, DH)
    return jnp.einsum(
        "rkgn,nkd->rkgd",
        weights.astype(jnp.bfloat16),
        value_three,
        preferred_element_type=jnp.float32,
    )


def on_device(queries, new_keys, new_values, cache_keys, cache_values, valid_len, block_of):
    here = jnp.reshape(lax.axis_index("seq"), (1,))
    rows_here = queries.shape[0]
    length = cache_keys.shape[0]
    heads = new_keys.shape[1] // DH
    own_block = lookup(block_of, here)[0]
    span_k, span_v = sent_together((new_keys, new_values), "seq", 0, 1)
    total = span_k.shape[0]
    every = jnp.arange(total, dtype=jnp.int32)
    span_pos = lookup(block_of, every // rows_here) * rows_here + every % rows_here
    own_pos = own_block * rows_here + jnp.arange(rows_here, dtype=jnp.int32)
    start_state = (
        jnp.full((rows_here, heads, GROUP), NEGATIVE, jnp.float32),
        jnp.zeros((rows_here, heads, GROUP, DH), jnp.float32),
        jnp.zeros((rows_here, heads, GROUP), jnp.float32),
    )
    pieces = (
        lax.all_gather(cache_keys, "seq", axis=0, tiled=True),
        lax.all_gather(cache_values, "seq", axis=0, tiled=True),
    )
    count = pieces[0].shape[0]
    many = count // length

    def inner(state, item):
        key_block, value_block, first = item
        shard = first // length
        block_k = lax.dynamic_slice_in_dim(span_k, shard * rows_here, rows_here, 0)
        block_v = lax.dynamic_slice_in_dim(span_v, shard * rows_here, rows_here, 0)
        block_pos = lax.dynamic_slice_in_dim(span_pos, shard * rows_here, rows_here, 0)
        filled = lookup(valid_len, jnp.reshape(shard, (1,)))[0]
        cache_live = jnp.arange(length, dtype=jnp.int32) < filled
        cache_seen = jnp.broadcast_to(cache_live[None, None, None, :], (rows_here, 1, 1, length))
        block_seen = visible(own_pos, block_pos, jnp.ones((rows_here,), bool))
        seen = jnp.concatenate([cache_seen, block_seen], -1)
        keys = jnp.concatenate([key_block, block_k], 0)
        values = jnp.concatenate([value_block, block_v], 0)
        scores = scores_of(queries, keys)
        local = masked_max(scores, seen)
        weights = weights_of(scores, seen, local)
        part_numer = accumulate(weights, values)
        part_total = jnp.sum(weights, axis=-1)
        best, sums, totals = state
        newest = jnp.maximum(best, local)
        keep = jnp.exp(best - newest)
        fresh = jnp.exp(local - newest)
        sums = sums * keep[..., None] + part_numer * fresh[..., None]
        totals = totals * keep + part_total * fresh
        return ((newest, sums, totals), None)

    firsts = length * jnp.arange(many, dtype=jnp.int32)
    state, _ = lax.scan(
        inner,
        start_state,
        (pieces[0].reshape(many, length, -1), pieces[1].reshape(many, length, -1), firsts),
    )
    final_top, numer, denom = state
    result = numer / denom[..., None]
    return result.reshape(rows_here, -1).astype(jnp.bfloat16)


def solution(mesh):
    placed = (
        P(("groups", "seq"), "head"),
        P(("groups", "seq"), "head"),
        P(("groups", "seq"), "head"),
        P(("groups", "seq"), "head"),
        P(("groups", "seq"), "head"),
        P("groups"),
        P("groups"),
    )
    return jax.shard_map(
        on_device,
        mesh=mesh,
        in_specs=placed,
        out_specs=P(("groups", "seq"), "head"),
        check_vma=False,
    )
```

profile of v0, /device:TPU:513, one launch (start us, length us, event | category | flops | bytes accessed | tf_op | source)
XLA Modules:
  0.0 292.7 jit_solution(12681562831767876139)
XLA Ops:
  9.0 1.3 broadcast_in_dim.92
  10.3 23.9 %all-to-all-start = ((bf16[16,128,256]{1,2,0:T(8,128)(2,1)}), bf16[16,128,256]{1,2,0:T(8,128)(2,1)S(1)}, u32[]{:S(2)}, u32[]{:S(2)}) async-start(bf16[16,128,256]{1,2,0:T(8,128)(2,1)} %broadcast_in_dim.92), calls=%async_computation | async-start | bytes 2097152 | tf_op jit(solution)/shard_map/all_to_all | solution.py:21
  34.2 1.4 fusion.47
  37.0 32.5 %all-to-all-done = bf16[16,128,256]{1,2,0:T(8,128)(2,1)S(1)} async-done(((bf16[16,128,256]{1,2,0:T(8,128)(2,1)}), bf16[16,128,256]{1,2,0:T(8,128)(2,1)S(1)}, u32[]{:S(2)}, u32[]{:S(2)}) %all-to-all-start) | async-done | bytes 1048608 | tf_op jit(solution)/shard_map/all_to_all | solution.py:21
  70.1 15.4 %all-gather.3.cloned.1.call-done = bf16[16384,128]{1,0:T(8,128)(2,1)} async-done(((bf16[1024,128]{1,0:T(8,128)(2,1)}), bf16[16384,128]{1,0:T(8,128)(2,1)}) %all-gather.3.cloned.1.call-update) | async-done | bytes 4194320 | tf_op jit(solution)/shard_map/all_gather | solution.py:94
  85.5 45.5 %all-gather.5.cloned.1.call-done = bf16[16384,128]{1,0:T(8,128)(2,1)} async-done(((bf16[1024,128]{1,0:T(8,128)(2,1)}), bf16[16384,128]{1,0:T(8,128)(2,1)}) %all-gather.5.cloned.1.call-update) | async-done | bytes 4194320 | tf_op jit(solution)/shard_map/all_gather | solution.py:95
  131.0 153.9 %while.17 = (s32[]{:T(128)}, f32[128,1,8]{0,2,1:T(8,128)S(1)}, f32[128,1,8,128]{0,3,2,1:T(8,128)S(1)}, f32[128,1,8]{0,2,1:T(8,128)S(1)}, s32[16]{0:T(128)S(1)}, ...) while((s32[]{:T(128)}, f32[128,1,8]{0,2,1:T(8,128)S(1)}, ...), condition=%wide.region_6.7_spmd.clone, body=%wide.region_2.6_spmd.clone.sunk | while | flops 616474816 | bytes 18533632 | solution.py:127
  139.5 1.1 fusion.65
  145.4 1.0 constant_dynamic-slice_fusion.6
  149.2 1.1 fusion.65
  158.8 1.1 fusion.65
  168.4 1.1 fusion.65
  178.0 1.1 fusion.65
  187.6 1.1 fusion.65
  197.3 1.1 fusion.65
  206.9 1.1 fusion.65
  216.5 1.1 fusion.65
  226.1 1.1 fusion.65
  235.8 1.1 fusion.65
  245.4 1.1 fusion.65
  255.0 1.1 fusion.65
  264.6 1.1 fusion.65
  274.2 1.1 fusion.65
  283.9 1.1 fusion.65
  (308 shorter events, 101.1 us)
Async XLA Ops:
  6.5 124.5 %copy-start.1 = (s32[16]{0:T(128)S(1)}, s32[16]{0:T(128)}, u32[]{:S(2)}) copy-start(s32[16]{0:T(128)} %param.14) | copy-start | bytes 196
  6.5 124.5 %copy-start = (bf16[128,1024]{1,0:T(8,128)(2,1)S(1)}, bf16[128,1024]{1,0:T(8,128)(2,1)}, u32[]{:S(2)}) copy-start(bf16[128,1024]{1,0:T(8,128)(2,1)} %param.9) | copy-start | bytes 786436
  6.6 78.9 %all-gather.3.cloned.1.call-start = ((), (), s32[]{:S(2)}) async-start(), calls=%async_computation.1 | async-start | bytes 4456448 | tf_op jit(solution)/shard_map/all_gather | solution.py:94
  7.3 123.7 %all-gather.5.cloned.1.call-start = ((), (), s32[]{:S(2)}) async-start(), calls=%async_computation.2 | async-start | bytes 4456448 | tf_op jit(solution)/shard_map/all_gather | solution.py:95
  10.3 59.2 %all-to-all-start = ((bf16[16,128,256]{1,2,0:T(8,128)(2,1)}), bf16[16,128,256]{1,2,0:T(8,128)(2,1)S(1)}, u32[]{:S(2)}, u32[]{:S(2)}) async-start(bf16[16,128,256]{1,2,0:T(8,128)(2,1)} %broadcast_in_dim.92), calls=%async_computation | async-start | bytes 2097152 | tf_op jit(solution)/shard_map/all_to_all | solution.py:21
Sparse Core Ops, SparseCore 0:
  9.2 76.2 all-gather.2
  87.3 43.6 all-gather.4
where the time goes:
time: 295 us; the launch traced here: 293 us
  waiting for transfers between devices  94.9 us (32%)
  local copies, waits for them, and re-layouts  49.1 us (17%)
  other arithmetic  40.9 us (14%)
  loops' own time  39 us (13%)
  matrix products  30.6 us (10%)
  starting transfers between devices  23.9 us (8%)
  between operations  14.2 us (5%)
    all_gather x1, waiting for transfers between devices, on_device(): lax.all_gather(cache_values, 'seq', axis=0, tiled=True)  45.5 us
    another operation x1, loops' own time, on_device(): lax.scan(inner, start_state, (pieces[0].reshape(many, length, -1), pieces...  39 us
    all_to_all x1, waiting for transfers between devices, from_everyone(): lax.all_to_all(jnp.broadcast_to(array[None], (size, *array.shape)), axis,...  32.5 us
    dynamic_slice x48, local copies, waits for them, and re-layouts, on_device(): lax.scan(inner, start_state, (pieces[0].reshape(many, length, -1), pieces...  27.4 us
    all_to_all x1, starting transfers between devices, from_everyone(): lax.all_to_all(jnp.broadcast_to(array[None], (size, *array.shape)), axis,...  23.9 us
    dot_general x16, matrix products, accumulate(): jnp.einsum('rkgn,nkd->rkgd', weights.astype(jnp.bfloat16), value_three, p...  17.5 us
    squeeze x16, local copies, waits for them, and re-layouts, on_device(): lax.scan(inner, start_state, (pieces[0].reshape(many, length, -1), pieces...  15.6 us
    all_gather x1, waiting for transfers between devices, on_device(): lax.all_gather(cache_keys, 'seq', axis=0, tiled=True)  15.4 us
  transfers between devices with their start and end apart: 3, of which 3 were waited for; matrix products, arithmetic and copies ran while one was open for 2% of the time, Pallas kernels for 0%

commit v1 on v0

v1 whole, which is shorter than its diff:
```python
import functools
import math

import jax
import jax.numpy as jnp
from jax import lax
from jax.experimental import pallas as pl
from jax.experimental.pallas import tpu as pltpu
from jax.sharding import PartitionSpec as P

DH = 128
GROUP = 8
NEGATIVE = -1e30
FACTOR = DH ** (-0.5) * math.log2(math.e)
WIDE = 256


def kernel(
    n,
    q_hbm, nk_hbm, nv_hbm, ck_hbm, cv_hbm, vl_ref, bo_ref,
    out_ref,
    kv, qs, s_ref, p_ref, acc, best, total,
    q_sem, own_sem, ring_send, ring_recv, pair_send, pair_recv,
):
    chips = n // 2
    far = chips // 2
    length = ck_hbm.shape[0]
    span = nk_hbm.shape[0]
    rows = length + span
    half = rows // 2
    me = lax.axis_index("seq")
    chip, core = me // 2, me % 2
    right = lax.rem(chip + 1, chips) * 2 + core
    left = lax.rem(chip + chips - 1, chips) * 2 + core
    pair = chip * 2 + 1 - core
    last = 2 * far - 1

    barrier = pltpu.get_barrier_semaphore()
    for peer in (right, left, pair):
        pl.semaphore_signal(
            barrier, inc=1, device_id={"seq": peer},
            device_id_type=pl.DeviceIdType.MESH,
        )

    def own_copies(part):
        cache, fresh = ((ck_hbm, nk_hbm), (cv_hbm, nv_hbm))[part]
        return (
            pltpu.make_async_copy(
                cache, kv.at[part, 0, 0, pl.ds(0, length)], own_sem.at[part, 0]
            ),
            pltpu.make_async_copy(
                fresh, kv.at[part, 0, 0, pl.ds(length, span)], own_sem.at[part, 1]
            ),
        )

    q_copies = [
        pltpu.make_async_copy(
            q_hbm.at[:, pl.ds(h * DH, DH)], qs.at[pl.ds(h * span, span)], q_sem.at[h]
        )
        for h in range(GROUP)
    ]
    for part in range(2):
        for c in own_copies(part):
            c.start()
    for c in q_copies:
        c.start()

    def ring(step, part, way):
        at = 0 if step == 1 else 2 * (step - 1) - 1 + way
        to = 2 * step - 1 + way if step < far else last
        first, count = (0, rows) if step < far else (way * half, half)
        return pltpu.make_async_remote_copy(
            src_ref=kv.at[part, 0, at, pl.ds(first, count)],
            dst_ref=kv.at[part, 0, to, pl.ds(first, count)],
            send_sem=ring_send.at[step - 1, part, way],
            recv_sem=ring_recv.at[step - 1, part, way],
            device_id={"seq": (right, left)[way]},
            device_id_type=pl.DeviceIdType.MESH,
        )

    def to_pair(at, part, way=0):
        first, count = (0, rows) if at < last else (way * half, half)
        return pltpu.make_async_remote_copy(
            src_ref=kv.at[part, 0, at, pl.ds(first, count)],
            dst_ref=kv.at[part, 1, at, pl.ds(first, count)],
            send_sem=pair_send.at[at + way, part],
            recv_sem=pair_recv.at[at + way, part],
            device_id={"seq": pair},
            device_id_type=pl.DeviceIdType.MESH,
        )

    acc[...] = jnp.zeros_like(acc)
    best[...] = jnp.full_like(best, NEGATIVE)
    total[...] = jnp.zeros_like(total)

    my_block = bo_ref[me]

    def process(side, at):
        dist = (at + 1) // 2
        offset = jnp.where(at % 2 == 1, chips - dist, dist)
        shard = lax.rem(chip + offset, chips) * 2 + lax.rem(core + side, 2)
        filled = vl_ref[shard]
        block = bo_ref[shard]
        slope = jnp.where(block == my_block, 1, 0)
        level = jnp.where(block < my_block, span - 1, jnp.where(block == my_block, 0, -1))
        at_row = lax.broadcasted_iota(jnp.int32, (rows, WIDE), 0)
        at_col = lax.broadcasted_iota(jnp.int32, (span, WIDE), 1) % span

        def columns(b, _):
            cols = pl.ds(pl.multiple_of(b * WIDE, WIDE), WIDE)
            s = lax.dot_general(
                kv[0, side, at], qs[cols, :], (((1,), (1,)), ((), ())),
                preferred_element_type=jnp.float32,
            )
            cache_seen = at_row[:length] < filled
            span_seen = at_row[:span] <= at_col * slope + level
            s_cache = jnp.where(cache_seen, s[:length], NEGATIVE)
            s_span = jnp.where(span_seen, s[length:], NEGATIVE)
            s_ref[:length, :] = s_cache
            s_ref[length:, :] = s_span
            local = jnp.maximum(
                jnp.max(s_cache, axis=0, keepdims=True),
                jnp.max(s_span, axis=0, keepdims=True),
            )
            w = jnp.exp2((s_ref[...] - local) * FACTOR)
            part_total = jnp.sum(w, axis=0, keepdims=True)
            p_ref[...] = w.astype(jnp.bfloat16)
            numer = lax.dot_general(
                kv[1, side, at], p_ref[...], (((0,), (0,)), ((), ())),
                preferred_element_type=jnp.float32,
            )
            old = best[:, cols]
            newest = jnp.maximum(old, local)
            keep = jnp.exp2((old - newest) * FACTOR)
            fresh = jnp.exp2((local - newest) * FACTOR)
            best[:, cols] = newest
            total[:, cols] = total[:, cols] * keep + part_total * fresh
            acc[:, cols] = acc[:, cols] * keep + numer * fresh
            return 0

        lax.fori_loop(0, GROUP * span // WIDE, columns, 0)

    def process_two(side, at):
        lax.fori_loop(0, 2, lambda i, _: (process(side, at + i), 0)[1], 0)

    pl.semaphore_wait(barrier, 3)
    for part in range(2):
        for c in own_copies(part):
            c.wait()
        for way in range(2):
            ring(1, part, way).start()
        to_pair(0, part).start()
    for c in q_copies:
        c.wait()
    process(0, 0)
    for part in range(2):
        to_pair(0, part).wait_recv()
    process(1, 0)
    for step in range(1, far):
        for part in range(2):
            for way in range(2):
                ring(step, part, way).wait_recv()
                if step + 1 < far or True:
                    if step + 1 <= far:
                        ring(step + 1, part, way).start()
                to_pair(2 * step - 1 + way, part).start()
        process_two(0, 2 * step - 1)
        for part in range(2):
            for way in range(2):
                to_pair(2 * step - 1 + way, part).wait_recv()
        process_two(1, 2 * step - 1)
    for part in range(2):
        for way in range(2):
            ring(far, part, way).wait_recv()
            to_pair(last, part, way).start()
    process(0, last)
    for part in range(2):
        for way in range(2):
            to_pair(last, part, way).wait_recv()
    process(1, last)

    for h in range(GROUP):
        cols = pl.ds(h * span, span)
        out_ref[:, pl.ds(h * DH, DH)] = (
            (acc[:, cols] / total[:, cols]).T.astype(out_ref.dtype)
        )

    for part in range(2):
        for step in range(1, far + 1):
            for way in range(2):
                ring(step, part, way).wait_send()
        for at in range(last):
            to_pair(at, part).wait_send()
        for way in range(2):
            to_pair(last, part, way).wait_send()


def solution(mesh):
    n = mesh.shape["seq"]

    def on_device(queries, new_keys, new_values, cache_keys, cache_values, valid_len, block_of):
        span = queries.shape[0]
        rows = cache_keys.shape[0] + span
        slots = n // 2
        any_spec = pl.BlockSpec(memory_space=pl.ANY)
        smem = pl.BlockSpec(memory_space=pltpu.SMEM)
        return pl.pallas_call(
            functools.partial(kernel, n),
            out_shape=jax.ShapeDtypeStruct(queries.shape, jnp.bfloat16),
            in_specs=[any_spec] * 5 + [smem] * 2,
            out_specs=pl.BlockSpec(memory_space=pltpu.VMEM),
            scratch_shapes=[
                pltpu.VMEM((2, 2, slots, rows, DH), jnp.bfloat16),
                pltpu.VMEM((GROUP * span, DH), jnp.bfloat16),
                pltpu.VMEM((rows, WIDE), jnp.float32),
                pltpu.VMEM((rows, WIDE), jnp.bfloat16),
                pltpu.VMEM((DH, GROUP * span), jnp.float32),
                pltpu.VMEM((1, GROUP * span), jnp.float32),
                pltpu.VMEM((1, GROUP * span), jnp.float32),
                pltpu.SemaphoreType.DMA((GROUP,)),
                pltpu.SemaphoreType.DMA((2, 2)),
                pltpu.SemaphoreType.DMA((slots // 2, 2, 2)),
                pltpu.SemaphoreType.DMA((slots // 2, 2, 2)),
                pltpu.SemaphoreType.DMA((slots + 1, 2)),
                pltpu.SemaphoreType.DMA((slots + 1, 2)),
            ],
            compiler_params=pltpu.CompilerParams(
                collective_id=0, has_side_effects=True,
                vmem_limit_bytes=60 * 1024 * 1024,
            ),
        )(queries, new_keys, new_values, cache_keys, cache_values, valid_len, block_of)

    rows_spec = P(("groups", "seq"), "head")
    return jax.shard_map(
        on_device,
        mesh=mesh,
        in_specs=(rows_spec,) * 5 + (P("groups"), P("groups")),
        out_specs=rows_spec,
        check_vma=False,
    )
```

time: 295 us -> 89 us (0.30)
  waiting for transfers between devices: 94.9 us -> 0 us
  Pallas kernels: 0 us -> 86.7 us
  local copies, waits for them, and re-layouts: 49.1 us -> 1.67 us
  other arithmetic: 40.9 us -> 0 us
  loops' own time: 39 us -> 0 us
  matrix products: 30.6 us -> 0 us
  starting transfers between devices: 23.9 us -> 0 us
  between operations: 14.2 us -> 0.01 us
    pallas_call x0 -> x1, Pallas kernels: none -> 86.7 us  [on_device(): pl.pallas_call(functools.partial(kernel, n), out_shape=jax.ShapeDtypeStru...]
    all_gather x2 -> x0, waiting for transfers between devices: 60.9 us -> none  [the longest x1 45.5 us: on_device(): lax.all_gather(cache_values, 'seq', axis=0, tiled=True)]
    another operation x1 -> x0, loops' own time: 39 us -> none  [on_device(): lax.scan(inner, start_state, (pieces[0].reshape(many, length, -1), pieces...]
    all_to_all x1 -> x0, waiting for transfers between devices: 32.5 us -> none  [from_everyone(): lax.all_to_all(jnp.broadcast_to(array[None], (size, *array.shape)), axis,...]
    dot_general x32 -> x0, matrix products: 30.6 us -> none  [the longest x16 17.5 us: accumulate(): jnp.einsum('rkgn,nkd->rkgd', weights.astype(jnp.bfloat16), value_three, p...]
    dynamic_slice x96 -> x0, local copies, waits for them, and re-layouts: 30.6 us -> none  [the longest x48 27.4 us: on_device(): lax.scan(inner, start_state, (pieces[0].reshape(many, length, -1), pieces...]
    reduce_sum x34 -> x0, other arithmetic: 25.4 us -> none  [the longest x16 13 us: inner(): part_total = jnp.sum(weights, axis=-1)]
    all_to_all x1 -> x0, starting transfers between devices: 23.9 us -> none  [from_everyone(): lax.all_to_all(jnp.broadcast_to(array[None], (size, *array.shape)), axis,...]
  transfers between devices with their start and end apart: 3 -> 0, of which waited for: 3 -> 0; matrix products, arithmetic and copies ran while one was open for 2% -> 0% of each run, Pallas kernels for 0% -> 0%
where the time goes in v1:
time: 89 us; the launch traced here: 88.4 us
  Pallas kernels  86.7 us (97%)
  local copies, waits for them, and re-layouts  1.67 us (2%)
    pallas_call x1, Pallas kernels, on_device(): pl.pallas_call(functools.partial(kernel, n), out_shape=jax.ShapeDtypeStru...  86.7 us

profile of v1, /device:TPU:513, one launch (start us, length us, event | category | flops | bytes accessed | tf_op | source)
XLA Modules:
  0.0 88.4 jit_solution(12691563874179456950)
XLA Ops:
  0.0 86.7 %shard_map.73 = bf16[128,1024]{1,0:T(8,128)(2,1)} custom-call(bf16[128,1024]{1,0:T(8,128)(2,1)} %q_hbm.1, bf16[128,128]{1,0:T(8,128)(2,1)} %nk_hbm.1, bf16[128,128]{1,0:T(8,128)(2,1)} %nv_hbm.1, bf16[1024,128]{1,0:T(8,128)(2,1)} %ck_hbm.1, bf16[1024,128]{1,0:T(8,128)(2,1)} %cv_hbm.1, s32[16]{0:T(128)} %vl_ref.1, s32[16]{0:T(128)} %bo_ref.1), custom_call_target="tpu_custom_call" | custom-call | tf_op jit(solution)/shard_map/pallas_call | solution.py:207
  86.7 1.7 %copy.9 = bf16[128,1024]{1,0:T(8,128)(2,1)} copy(bf16[128,1024]{1,0:T(8,128)(2,1)} %shard_map.73) | data formatting | bytes 524288

commit v2 on v1

v2 whole, which is shorter than its diff:
```python
import functools
import math

import jax
import jax.numpy as jnp
from jax import lax
from jax.experimental import pallas as pl
from jax.experimental.pallas import tpu as pltpu
from jax.sharding import PartitionSpec as P

DH = 128
GROUP = 8
NEGATIVE = -1e30
FACTOR = DH ** (-0.5) * math.log2(math.e)
WIDE = 256
TALL = 384


def kernel(
    n,
    q_hbm, nk_hbm, nv_hbm, ck_hbm, cv_hbm, vl_ref, bo_ref,
    out_ref,
    kv, qs, vt, bias, s_ref, weights, tops, parts, acc, best, total,
    hello, q_sem, own_sem, ring_send, ring_recv, pair_send, pair_recv,
):
    chips = n // 2
    far = chips // 2
    length = ck_hbm.shape[0]
    span = nk_hbm.shape[0]
    rows = length + span
    half = rows // 2
    me = lax.axis_index("seq")
    chip, core = me // 2, me % 2
    right = lax.rem(chip + 1, chips) * 2 + core
    left = lax.rem(chip + chips - 1, chips) * 2 + core
    pair = chip * 2 + 1 - core
    last = 2 * far - 1

    barrier = pltpu.get_barrier_semaphore()

    def greet(peer):
        pl.semaphore_signal(
            barrier, inc=1, device_id={"seq": peer}, device_id_type=pl.DeviceIdType.MESH
        )

    greet(right)
    greet(left)
    pl.when(core == 1)(lambda: greet(pair))

    def own_copies(part):
        cache, fresh = ((ck_hbm, nk_hbm), (cv_hbm, nv_hbm))[part]
        return (
            pltpu.make_async_copy(
                cache, kv.at[part, 0, 0, pl.ds(0, length)], own_sem.at[part, 0]
            ),
            pltpu.make_async_copy(
                fresh, kv.at[part, 0, 0, pl.ds(length, span)], own_sem.at[part, 1]
            ),
        )

    q_copies = [
        pltpu.make_async_copy(
            q_hbm.at[:, pl.ds(h * DH, DH)],
            qs.at[pl.ds(h * span, span), pl.ds(0, DH)],
            q_sem.at[h],
        )
        for h in range(GROUP)
    ]
    for part in range(2):
        for c in own_copies(part):
            c.start()
    for c in q_copies:
        c.start()

    def ring(step, part, way):
        at = 0 if step == 1 else 2 * (step - 1) - 1 + way
        to = 2 * step - 1 + way if step < far else last
        first, count = (0, rows) if step < far else (way * half, half)
        return pltpu.make_async_remote_copy(
            src_ref=kv.at[part, 0, at, pl.ds(first, count)],
            dst_ref=kv.at[part, 0, to, pl.ds(first, count)],
            send_sem=ring_send.at[step - 1, part, way],
            recv_sem=ring_recv.at[step - 1, part, way],
            device_id={"seq": (right, left)[way]},
            device_id_type=pl.DeviceIdType.MESH,
        )

    def to_pair(at, part, way=0):
        first, count = (way * half, half) if at is last else (0, rows)
        return pltpu.make_async_remote_copy(
            src_ref=kv.at[part, 0, at, pl.ds(first, count)],
            dst_ref=kv.at[part, 1, at, pl.ds(first, count)],
            send_sem=pair_send.at[at + way, part],
            recv_sem=pair_recv.at[at + way, part],
            device_id={"seq": pair},
            device_id_type=pl.DeviceIdType.MESH,
        )

    acc[...] = jnp.zeros_like(acc)
    best[...] = jnp.full_like(best, NEGATIVE)
    total[...] = jnp.zeros_like(total)
    place = lax.broadcasted_iota(jnp.int32, (span, DH), 0)
    lane = lax.broadcasted_iota(jnp.int32, (span, DH), 1)
    marks = jnp.where((lane > place) | (lane == 0), 1.0, 0.0).astype(jnp.bfloat16)
    for h in range(GROUP):
        qs[pl.ds(h * span, span), pl.ds(DH, DH)] = marks

    my_block = bo_ref[me]
    blocks = GROUP * span // WIDE

    def attend(side, at, weigh_into, finish):
        dist = (at + 1) // 2
        offset = jnp.where(at % 2 == 1, chips - dist, dist)
        shard = lax.rem(chip + offset, chips) * 2 + lax.rem(core + side, 2)
        filled = vl_ref[shard]
        block = bo_ref[shard]
        row = lax.broadcasted_iota(jnp.int32, (length, DH), 0)
        col = lax.broadcasted_iota(jnp.int32, (length, DH), 1)
        bias[pl.ds(0, length), :] = jnp.where(
            (col == 0) & (row >= filled), NEGATIVE, 0.0
        ).astype(jnp.bfloat16)
        hidden_col = jnp.where(block == my_block, place, jnp.where(block < my_block, -1, 0))
        hidden = (lane == hidden_col) & ((place > 0) | (block > my_block))
        bias[pl.ds(length, span), :] = jnp.where(hidden, NEGATIVE, 0.0).astype(jnp.bfloat16)

        local, sums = {}, {}

        def score(b, first):
            s = lax.dot_general(
                jnp.concatenate(
                    [kv[0, side, at, pl.ds(first, TALL), :], bias[pl.ds(first, TALL), :]], axis=1
                ),
                qs[pl.ds(b * WIDE, WIDE), :],
                (((1,), (1,)), ((), ())),
                preferred_element_type=jnp.float32,
            )
            s_ref[pl.ds(first, TALL), :] = s
            high = jnp.max(s.reshape(TALL // 8, 8, WIDE), axis=0)
            local[b] = jnp.maximum(local[b], high) if b in local else high

        def weigh(b, first):
            w = jnp.exp2((s_ref[pl.ds(first, span), :] - local[b]) * FACTOR)
            part = jnp.sum(w.reshape(span // 8, 8, WIDE), axis=0)
            sums[b] = sums[b] + part if b in sums else part
            weigh_into(b)[pl.ds(first, span), :] = w.astype(jnp.bfloat16)

        for b in range(blocks + 1):
            for first in range(0, rows, TALL):
                if b > 0:
                    for inner in range(first, first + TALL, span):
                        weigh(b - 1, inner)
                if b < blocks:
                    score(b, first)
            if b < blocks:
                local[b] = jnp.max(local[b], axis=0, keepdims=True)
            if b > 0:
                finish(b - 1, local[b - 1], jnp.sum(sums[b - 1], axis=0, keepdims=True))

    def combine(b, weighted, local, part_total):
        cols = pl.ds(b * WIDE, WIDE)
        numer = jnp.dot(vt[...], weighted, preferred_element_type=jnp.float32)
        old = best[:, cols]
        newest = jnp.maximum(old, local)
        keep = jnp.exp2((old - newest) * FACTOR)
        fresh = jnp.exp2((local - newest) * FACTOR)
        best[:, cols] = newest
        total[:, cols] = total[:, cols] * keep + part_total * fresh
        acc[:, cols] = acc[:, cols] * keep + numer * fresh

    def weigh_shard(side, at):
        def finish(b, local, part_total):
            cols = pl.ds(b * WIDE, WIDE)
            tops[side, at, :, cols] = local
            parts[side, at, :, cols] = part_total

        attend(side, at, lambda b: weights.at[side, at, b], finish)

    def combine_shard(side, at):
        vt[...] = kv[1, side, at].T
        for b in range(blocks):
            cols = pl.ds(b * WIDE, WIDE)
            combine(b, weights[side, at, b], tops[side, at, :, cols], parts[side, at, :, cols])

    def receive(step, part):
        for way in (1, 0):
            ring(step, part, way).wait_recv()
            if step < far:
                ring(step + 1, part, way).start()
        for way in (1, 0):
            if step < far:
                if step > 1:
                    to_pair(2 * step - 1 + way, part).start()
            else:
                to_pair(last, part, way).start()

    def met_pair():
        receive(1, 1)

        @pl.when(core == 1)
        def _():
            pl.semaphore_wait(hello, 1)
            for part in range(2):
                to_pair(0, part).start()

        for at in (2, 1):
            for part in range(2):
                to_pair(at, part).start()

    def last_of_pair(part):
        for way in range(2):
            to_pair(last, part, way).wait_recv()

    turns = []

    def turn(what, side, at, action=None):
        turns.append((what, side, at, action))

    turn(0, 0, 0)
    turn(1, 0, 0)
    turn(0, 0, 2, lambda: receive(1, 0))
    turn(0, 0, 1)
    turn(1, 0, 2, met_pair)
    turn(1, 0, 1)
    turn(0, 1, 0)
    turn(1, 1, 0)
    behind = []
    for step in range(2, far):
        new = [2 * step, 2 * step - 1]
        turn(0, 0, new[0], functools.partial(receive, step, 0))
        turn(0, 0, new[1])
        for at in behind:
            turn(0, 1, at)
        if step + 1 == far and far > 2 and step > 2:
            turn(0, 1, new[0])
            early = [new[0]]
        else:
            early = []
        turn(1, 0, new[0], functools.partial(receive, step, 1))
        turn(1, 0, new[1])
        for at in [2 * step - 2] * (step > 2) + behind + early:
            turn(1, 1, at)
        if step + 1 < far:
            for at in (2 * step - 2, 2 * step - 3):
                turn(0, 1, at)
                turn(1, 1, at)
            turn(0, 1, new[0])
            behind = [new[1]]
        else:
            for at in new:
                if at not in early:
                    turn(0, 1, at)
                    turn(1, 1, at)
    turn(0, 0, last, lambda: receive(far, 0))
    turn(0, 1, last, lambda: last_of_pair(0))
    turn(1, 0, last, lambda: receive(far, 1))
    turn(1, 1, last, lambda: last_of_pair(1))

    def one(i, _):
        what = i * 0
        side = i * 0
        at = i * 0
        for k, (w, a, b, action) in enumerate(turns):
            what = jnp.where(i == k, w, what)
            side = jnp.where(i == k, a, side)
            at = jnp.where(i == k, b, at)
            if action is not None:
                pl.when(i == k)(action)

        for part in range(2):

            @pl.when((what == part) & (side == 1) & (at != last))
            def _():
                to_pair(at, part).wait_recv()

        pl.when(what == 0)(lambda: weigh_shard(side, at))
        pl.when(what == 1)(lambda: combine_shard(side, at))
        return 0

    pl.semaphore_wait(barrier, 3 - core)

    @pl.when(core == 0)
    def _():
        pl.semaphore_signal(
            hello, inc=1, device_id={"seq": pair}, device_id_type=pl.DeviceIdType.MESH
        )

    for part in range(2):
        for c in own_copies(part):
            c.wait()
        for way in range(2):
            ring(1, part, way).start()

    @pl.when(core == 0)
    def _():
        for part in range(2):
            to_pair(0, part).start()

    for c in q_copies:
        c.wait()
    lax.fori_loop(0, len(turns), one, 0)

    for h in range(GROUP):
        cols = pl.ds(h * span, span)
        out_ref[:, pl.ds(h * DH, DH)] = (
            (acc[:, cols] / total[:, cols]).T.astype(out_ref.dtype)
        )

    for part in range(2):
        for step in range(1, far + 1):
            for way in range(2):
                ring(step, part, way).wait_send()
        for at in range(last):
            to_pair(at, part).wait_send()
        for way in range(2):
            to_pair(last, part, way).wait_send()


def solution(mesh):
    n = mesh.shape["seq"]

    def on_device(queries, new_keys, new_values, cache_keys, cache_values, valid_len, block_of):
        span = queries.shape[0]
        rows = cache_keys.shape[0] + span
        slots = n // 2
        any_spec = pl.BlockSpec(memory_space=pl.ANY)
        smem = pl.BlockSpec(memory_space=pltpu.SMEM)
        return pl.pallas_call(
            functools.partial(kernel, n),
            out_shape=jax.ShapeDtypeStruct(queries.shape, jnp.bfloat16),
            in_specs=[any_spec] * 5 + [smem] * 2,
            out_specs=pl.BlockSpec(memory_space=pltpu.VMEM),
            scratch_shapes=[
                pltpu.VMEM((2, 2, slots, rows, DH), jnp.bfloat16),
                pltpu.VMEM((GROUP * span, 2 * DH), jnp.bfloat16),
                pltpu.VMEM((DH, rows), jnp.bfloat16),
                pltpu.VMEM((rows, DH), jnp.bfloat16),
                pltpu.VMEM((rows, WIDE), jnp.float32),
                pltpu.VMEM((2, slots, GROUP * span // WIDE, rows, WIDE), jnp.bfloat16),
                pltpu.VMEM((2, slots, 1, GROUP * span), jnp.float32),
                pltpu.VMEM((2, slots, 1, GROUP * span), jnp.float32),
                pltpu.VMEM((DH, GROUP * span), jnp.float32),
                pltpu.VMEM((1, GROUP * span), jnp.float32),
                pltpu.VMEM((1, GROUP * span), jnp.float32),
                pltpu.SemaphoreType.REGULAR,
                pltpu.SemaphoreType.DMA((GROUP,)),
                pltpu.SemaphoreType.DMA((2, 2)),
                pltpu.SemaphoreType.DMA((slots // 2, 2, 2)),
                pltpu.SemaphoreType.DMA((slots // 2, 2, 2)),
                pltpu.SemaphoreType.DMA((slots + 1, 2)),
                pltpu.SemaphoreType.DMA((slots + 1, 2)),
            ],
            compiler_params=pltpu.CompilerParams(
                collective_id=0, has_side_effects=True,
                vmem_limit_bytes=60 * 1024 * 1024,
            ),
        )(queries, new_keys, new_values, cache_keys, cache_values, valid_len, block_of)

    rows_spec = P(("groups", "seq"), "head")
    return jax.shard_map(
        on_device,
        mesh=mesh,
        in_specs=(rows_spec,) * 5 + (P("groups"), P("groups")),
        out_specs=rows_spec,
        check_vma=False,
    )
```

time: 89 us -> 76.2 us (0.86)
  Pallas kernels: 86.7 us -> 74.4 us
    pallas_call x1, Pallas kernels: 86.7 us -> 74.4 us  [on_device(): pl.pallas_call(functools.partial(kernel, n), out_shape=jax.ShapeDtypeStru...]
where the time goes in v2:
time: 76.2 us; the launch traced here: 76.1 us
  Pallas kernels  74.4 us (98%)
  local copies, waits for them, and re-layouts  1.67 us (2%)
    pallas_call x1, Pallas kernels, on_device(): pl.pallas_call(functools.partial(kernel, n), out_shape=jax.ShapeDtypeStru...  74.4 us
    unnamed x1, local copies, waits for them, and re-layouts  1.67 us

profile of v2, /device:TPU:513, one launch (start us, length us, event | category | flops | bytes accessed | tf_op | source)
XLA Modules:
  0.0 76.1 jit_solution(18405108633218120450)
XLA Ops:
  0.0 74.4 %shard_map.73 = bf16[128,1024]{1,0:T(8,128)(2,1)} custom-call(bf16[128,1024]{1,0:T(8,128)(2,1)} %q_hbm.1, bf16[128,128]{1,0:T(8,128)(2,1)} %nk_hbm.1, bf16[128,128]{1,0:T(8,128)(2,1)} %nv_hbm.1, bf16[1024,128]{1,0:T(8,128)(2,1)} %ck_hbm.1, bf16[1024,128]{1,0:T(8,128)(2,1)} %cv_hbm.1, s32[16]{0:T(128)} %vl_ref.1, s32[16]{0:T(128)} %bo_ref.1), custom_call_target="tpu_custom_call" | custom-call | tf_op jit(solution)/shard_map/pallas_call | solution.py:327
  74.4 1.7 %copy.9 = bf16[128,1024]{1,0:T(8,128)(2,1)} copy(bf16[128,1024]{1,0:T(8,128)(2,1)} %shard_map.73) | data formatting | bytes 524288

commit v3 on v2

--- a/solution.py
+++ b/solution.py
@@ -15,12 +15,41 @@
 WIDE = 256
 TALL = 384
 
+TURNS = (
+    (
+        (3, 0,),
+        (17, 9,),
+        (18, 10, 7, 23,),
+        (33, 25, 15,),
+        (34, 26, 39, 31,),
+        (49, 41, 53, 45,),
+        (50, 42, 54, 46,),
+        (57,),
+        (61,),
+        (58,),
+        (62,),
+    ),
+    (
+        (3, 7,),
+        (17, 9,),
+        (18, 10, 23, 0,),
+        (33, 25, 15,),
+        (34, 26, 39, 31,),
+        (49, 41, 53, 45,),
+        (50, 42, 54, 46,),
+        (57,),
+        (61,),
+        (58,),
+        (62,),
+    ),
+)
+
 
 def kernel(
     n,
     q_hbm, nk_hbm, nv_hbm, ck_hbm, cv_hbm, vl_ref, bo_ref,
     out_ref,
-    kv, qs, vt, bias, s_ref, weights, tops, parts, acc, best, total,
+    kv, qs, vt, bias, s_ref, p_even, p_odd, weights, tops, parts, acc, best, total,
     hello, q_sem, own_sem, ring_send, ring_recv, pair_send, pair_recv,
 ):
     chips = n // 2
@@ -107,6 +136,7 @@
 
     my_block = bo_ref[me]
     blocks = GROUP * span // WIDE
+    p_refs = (p_even, p_odd)
 
     def attend(side, at, weigh_into, finish):
         dist = (at + 1) // 2
@@ -181,17 +211,34 @@
             cols = pl.ds(b * WIDE, WIDE)
             combine(b, weights[side, at, b], tops[side, at, :, cols], parts[side, at, :, cols])
 
+    def whole_shard(side, at):
+        waiting = []
+        vt[...] = kv[1, side, at].T
+
+        def drain():
+            b, local, part_total = waiting.pop(0)
+            combine(b, p_refs[b % 2][...], local, part_total)
+
+        def finish(b, local, part_total):
+            waiting.append((b, local, part_total))
+            if len(waiting) > 1:
+                drain()
+
+        attend(side, at, lambda b: p_refs[b % 2], finish)
+        drain()
+
     def receive(step, part):
         for way in (1, 0):
+            at = 2 * step - 1 + way if step < far else last
             ring(step, part, way).wait_recv()
             if step < far:
                 ring(step + 1, part, way).start()
-        for way in (1, 0):
-            if step < far:
-                if step > 1:
-                    to_pair(2 * step - 1 + way, part).start()
+            if step == far:
+                to_pair(at, part, way).start()
+            elif step > 1:
+                to_pair(at, part).start()
             else:
-                to_pair(last, part, way).start()
+                pl.when(core == 0)(to_pair(at, part).start)
 
     def met_pair():
         receive(1, 1)
@@ -199,81 +246,49 @@
         @pl.when(core == 1)
         def _():
             pl.semaphore_wait(hello, 1)
-            for part in range(2):
-                to_pair(0, part).start()
-
-        for at in (2, 1):
-            for part in range(2):
-                to_pair(at, part).start()
+            for at in (0, 2, 1):
+                for part in range(2):
+                    to_pair(at, part).start()
 
     def last_of_pair(part):
         for way in range(2):
             to_pair(last, part, way).wait_recv()
 
+    actions = [
+        None,
+        lambda: receive(1, 0), met_pair,
+        lambda: receive(2, 0), lambda: receive(2, 1),
+        lambda: receive(3, 0), lambda: receive(3, 1),
+        lambda: receive(4, 0), lambda: last_of_pair(0),
+        lambda: receive(4, 1), lambda: last_of_pair(1),
+    ]
     turns = []
-
-    def turn(what, side, at, action=None):
-        turns.append((what, side, at, action))
-
-    turn(0, 0, 0)
-    turn(1, 0, 0)
-    turn(0, 0, 2, lambda: receive(1, 0))
-    turn(0, 0, 1)
-    turn(1, 0, 2, met_pair)
-    turn(1, 0, 1)
-    turn(0, 1, 0)
-    turn(1, 1, 0)
-    behind = []
-    for step in range(2, far):
-        new = [2 * step, 2 * step - 1]
-        turn(0, 0, new[0], functools.partial(receive, step, 0))
-        turn(0, 0, new[1])
-        for at in behind:
-            turn(0, 1, at)
-        if step + 1 == far and far > 2 and step > 2:
-            turn(0, 1, new[0])
-            early = [new[0]]
-        else:
-            early = []
-        turn(1, 0, new[0], functools.partial(receive, step, 1))
-        turn(1, 0, new[1])
-        for at in [2 * step - 2] * (step > 2) + behind + early:
-            turn(1, 1, at)
-        if step + 1 < far:
-            for at in (2 * step - 2, 2 * step - 3):
-                turn(0, 1, at)
-                turn(1, 1, at)
-            turn(0, 1, new[0])
-            behind = [new[1]]
-        else:
-            for at in new:
-                if at not in early:
-                    turn(0, 1, at)
-                    turn(1, 1, at)
-    turn(0, 0, last, lambda: receive(far, 0))
-    turn(0, 1, last, lambda: last_of_pair(0))
-    turn(1, 0, last, lambda: receive(far, 1))
-    turn(1, 1, last, lambda: last_of_pair(1))
+    for action, zero, one in zip(actions, TURNS[0], TURNS[1], strict=True):
+        for k, both in enumerate(zip(zero, one, strict=True)):
+            turns.append((*((t % 4, t // 4 % 2, t // 8) for t in both), None if k else action))
 
     def one(i, _):
-        what = i * 0
-        side = i * 0
-        at = i * 0
-        for k, (w, a, b, action) in enumerate(turns):
-            what = jnp.where(i == k, w, what)
-            side = jnp.where(i == k, a, side)
-            at = jnp.where(i == k, b, at)
+        def pick(field):
+            found = i * 0
+            for k, (zero, one, _) in enumerate(turns):
+                value = jnp.where(core == 1, one[field], zero[field])
+                found = jnp.where(i == k, value, found)
+            return found
+
+        what, side, at = pick(0), pick(1), pick(2)
+        for k, (_, _, action) in enumerate(turns):
             if action is not None:
                 pl.when(i == k)(action)
 
         for part in range(2):
 
-            @pl.when((what == part) & (side == 1) & (at != last))
+            @pl.when(((what == part + 1) | (what == 3)) & (side == 1) & (at != last))
             def _():
                 to_pair(at, part).wait_recv()
 
-        pl.when(what == 0)(lambda: weigh_shard(side, at))
-        pl.when(what == 1)(lambda: combine_shard(side, at))
+        pl.when(what == 1)(lambda: weigh_shard(side, at))
+        pl.when(what == 2)(lambda: combine_shard(side, at))
+        pl.when(what == 3)(lambda: whole_shard(side, at))
         return 0
 
     pl.semaphore_wait(barrier, 3 - core)
@@ -335,6 +350,8 @@
                 pltpu.VMEM((DH, rows), jnp.bfloat16),
                 pltpu.VMEM((rows, DH), jnp.bfloat16),
                 pltpu.VMEM((rows, WIDE), jnp.float32),
+                pltpu.VMEM((rows, WIDE), jnp.bfloat16),
+                pltpu.VMEM((rows, WIDE), jnp.bfloat16),
                 pltpu.VMEM((2, slots, GROUP * span // WIDE, rows, WIDE), jnp.bfloat16),
                 pltpu.VMEM((2, slots, 1, GROUP * span), jnp.float32),
                 pltpu.VMEM((2, slots, 1, GROUP * span), jnp.float32),

time: 76.2 us -> 70.6 us (0.927)
  Pallas kernels: 74.4 us -> 68.8 us
    pallas_call x1, Pallas kernels: 74.4 us -> 68.8 us  [on_device(): pl.pallas_call(functools.partial(kernel, n), out_shape=jax.ShapeDtypeStru...]
where the time goes in v3:
time: 70.6 us; the launch traced here: 70.5 us
  Pallas kernels  68.8 us (97%)
  local copies, waits for them, and re-layouts  1.67 us (2%)
    pallas_call x1, Pallas kernels, on_device(): pl.pallas_call(functools.partial(kernel, n), out_shape=jax.ShapeDtypeStru...  68.8 us
    unnamed x1, local copies, waits for them, and re-layouts  1.67 us

profile of v3, /device:TPU:513, one launch (start us, length us, event | category | flops | bytes accessed | tf_op | source)
XLA Modules:
  0.0 70.5 jit_solution(14482721130189362550)
XLA Ops:
  0.0 68.8 %shard_map.73 = bf16[128,1024]{1,0:T(8,128)(2,1)} custom-call(bf16[128,1024]{1,0:T(8,128)(2,1)} %q_hbm.1, bf16[128,128]{1,0:T(8,128)(2,1)} %nk_hbm.1, bf16[128,128]{1,0:T(8,128)(2,1)} %nv_hbm.1, bf16[1024,128]{1,0:T(8,128)(2,1)} %ck_hbm.1, bf16[1024,128]{1,0:T(8,128)(2,1)} %cv_hbm.1, s32[16]{0:T(128)} %vl_ref.1, s32[16]{0:T(128)} %bo_ref.1), custom_call_target="tpu_custom_call" | custom-call | tf_op jit(solution)/shard_map/pallas_call | solution.py:342
  68.8 1.7 %copy.9 = bf16[128,1024]{1,0:T(8,128)(2,1)} copy(bf16[128,1024]{1,0:T(8,128)(2,1)} %shard_map.73) | data formatting | bytes 524288

commit v4 on v3

--- a/solution.py
+++ b/solution.py
@@ -17,10 +17,11 @@
 
 TURNS = (
     (
-        (3, 0,),
+        (3,),
+        (7,),
         (17, 9,),
-        (18, 10, 7, 23,),
-        (33, 25, 15,),
+        (18, 10, 23, 15,),
+        (33, 25,),
         (34, 26, 39, 31,),
         (49, 41, 53, 45,),
         (50, 42, 54, 46,),
@@ -30,10 +31,11 @@
         (62,),
     ),
     (
-        (3, 7,),
+        (3,),
+        (7,),
         (17, 9,),
-        (18, 10, 23, 0,),
-        (33, 25, 15,),
+        (18, 10, 23, 15,),
+        (33, 25,),
         (34, 26, 39, 31,),
         (49, 41, 53, 45,),
         (50, 42, 54, 46,),
@@ -203,13 +205,13 @@
             tops[side, at, :, cols] = local
             parts[side, at, :, cols] = part_total
 
-        attend(side, at, lambda b: weights.at[side, at, b], finish)
+        attend(side, at, lambda b: weights.at[at + side * 3, b], finish)
 
     def combine_shard(side, at):
         vt[...] = kv[1, side, at].T
         for b in range(blocks):
             cols = pl.ds(b * WIDE, WIDE)
-            combine(b, weights[side, at, b], tops[side, at, :, cols], parts[side, at, :, cols])
+            combine(b, weights[at + side * 3, b], tops[side, at, :, cols], parts[side, at, :, cols])
 
     def whole_shard(side, at):
         waiting = []
@@ -235,28 +237,23 @@
                 ring(step + 1, part, way).start()
             if step == far:
                 to_pair(at, part, way).start()
-            elif step > 1:
+            else:
                 to_pair(at, part).start()
-            else:
-                pl.when(core == 0)(to_pair(at, part).start)
-
-    def met_pair():
-        receive(1, 1)
-
+
+    def meet_pair():
         @pl.when(core == 1)
         def _():
             pl.semaphore_wait(hello, 1)
-            for at in (0, 2, 1):
-                for part in range(2):
-                    to_pair(at, part).start()
+            for part in range(2):
+                to_pair(0, part).start()
 
     def last_of_pair(part):
         for way in range(2):
             to_pair(last, part, way).wait_recv()
 
     actions = [
-        None,
-        lambda: receive(1, 0), met_pair,
+        None, meet_pair,
+        lambda: receive(1, 0), lambda: receive(1, 1),
         lambda: receive(2, 0), lambda: receive(2, 1),
         lambda: receive(3, 0), lambda: receive(3, 1),
         lambda: receive(4, 0), lambda: last_of_pair(0),
@@ -337,11 +334,11 @@
         span = queries.shape[0]
         rows = cache_keys.shape[0] + span
         slots = n // 2
-        any_spec = pl.BlockSpec(memory_space=pl.ANY)
+        any_spec = pl.BlockSpec(memory_space=pltpu.HBM)
         smem = pl.BlockSpec(memory_space=pltpu.SMEM)
         return pl.pallas_call(
             functools.partial(kernel, n),
-            out_shape=jax.ShapeDtypeStruct(queries.shape, jnp.bfloat16),
+            out_shape=pltpu.VMEM(queries.shape, jnp.bfloat16),
             in_specs=[any_spec] * 5 + [smem] * 2,
             out_specs=pl.BlockSpec(memory_space=pltpu.VMEM),
             scratch_shapes=[
@@ -352,7 +349,7 @@
                 pltpu.VMEM((rows, WIDE), jnp.float32),
                 pltpu.VMEM((rows, WIDE), jnp.bfloat16),
                 pltpu.VMEM((rows, WIDE), jnp.bfloat16),
-                pltpu.VMEM((2, slots, GROUP * span // WIDE, rows, WIDE), jnp.bfloat16),
+                pltpu.VMEM((slots + 3, GROUP * span // WIDE, rows, WIDE), jnp.bfloat16),
                 pltpu.VMEM((2, slots, 1, GROUP * span), jnp.float32),
                 pltpu.VMEM((2, slots, 1, GROUP * span), jnp.float32),
                 pltpu.VMEM((DH, GROUP * span), jnp.float32),

time: 70.6 us -> 68.2 us (0.966)
  Pallas kernels: 68.8 us -> 67.4 us
  local copies, waits for them, and re-layouts: 1.67 us -> 0.71 us
    pallas_call x1, Pallas kernels: 68.8 us -> 67.4 us  [on_device(): pl.pallas_call(functools.partial(kernel, n), out_shape=pltpu.VMEM(queries...]
    unnamed x1, local copies, waits for them, and re-layouts: 1.67 us -> 0.71 us
where the time goes in v4:
time: 68.2 us; the launch traced here: 68.1 us
  Pallas kernels  67.4 us (99%)
  local copies, waits for them, and re-layouts  0.71 us (1%)
    pallas_call x1, Pallas kernels, on_device(): pl.pallas_call(functools.partial(kernel, n), out_shape=pltpu.VMEM(queries...  67.4 us

profile of v4, /device:TPU:513, one launch (start us, length us, event | category | flops | bytes accessed | tf_op | source)
XLA Modules:
  0.0 68.1 jit_solution(5206254805124821137)
XLA Ops:
  0.0 67.4 %shard_map.73 = bf16[128,1024]{1,0:T(8,128)(2,1)S(1)} custom-call(bf16[128,1024]{1,0:T(8,128)(2,1)} %q_hbm.1, bf16[128,128]{1,0:T(8,128)(2,1)} %nk_hbm.1, bf16[128,128]{1,0:T(8,128)(2,1)} %nv_hbm.1, bf16[1024,128]{1,0:T(8,128)(2,1)} %ck_hbm.1, bf16[1024,128]{1,0:T(8,128)(2,1)} %cv_hbm.1, s32[16]{0:T(128)} %vl_ref.1, s32[16]{0:T(128)} %bo_ref.1), custom_call_target="tpu_custom_call" | custom-call | tf_op jit(solution)/shard_map/pallas_call | solution.py:339
  67.4 0.7 %copy.9 = bf16[128,1024]{1,0:T(8,128)(2,1)} copy(bf16[128,1024]{1,0:T(8,128)(2,1)S(1)} %shard_map.73) | data formatting | bytes 524288

commit v5 on v4

--- a/solution.py
+++ b/solution.py
@@ -18,8 +18,8 @@
 TURNS = (
     (
         (3,),
+        (17, 9,),
         (7,),
-        (17, 9,),
         (18, 10, 23, 15,),
         (33, 25,),
         (34, 26, 39, 31,),
@@ -32,8 +32,8 @@
     ),
     (
         (3,),
+        (17, 9,),
         (7,),
-        (17, 9,),
         (18, 10, 23, 15,),
         (33, 25,),
         (34, 26, 39, 31,),
@@ -237,6 +237,8 @@
                 ring(step + 1, part, way).start()
             if step == far:
                 to_pair(at, part, way).start()
+            elif step == 1 and part == 0:
+                pl.when(core == 0)(to_pair(at, part).start)
             else:
                 to_pair(at, part).start()
 
@@ -244,16 +246,16 @@
         @pl.when(core == 1)
         def _():
             pl.semaphore_wait(hello, 1)
-            for part in range(2):
-                to_pair(0, part).start()
+            for at, part in ((0, 0), (0, 1), (2, 0), (1, 0)):
+                to_pair(at, part).start()
 
     def last_of_pair(part):
         for way in range(2):
             to_pair(last, part, way).wait_recv()
 
     actions = [
-        None, meet_pair,
-        lambda: receive(1, 0), lambda: receive(1, 1),
+        None, lambda: receive(1, 0),
+        meet_pair, lambda: receive(1, 1),
         lambda: receive(2, 0), lambda: receive(2, 1),
         lambda: receive(3, 0), lambda: receive(3, 1),
         lambda: receive(4, 0), lambda: last_of_pair(0),

time: 68.2 us -> 65.2 us (0.956)
  Pallas kernels: 67.4 us -> 64.3 us
    pallas_call x1, Pallas kernels: 67.4 us -> 64.3 us  [on_device(): pl.pallas_call(functools.partial(kernel, n), out_shape=pltpu.VMEM(queries...]
where the time goes in v5:
time: 65.2 us; the launch traced here: 65.1 us
  Pallas kernels  64.3 us (99%)
  local copies, waits for them, and re-layouts  0.71 us (1%)
    pallas_call x1, Pallas kernels, on_device(): pl.pallas_call(functools.partial(kernel, n), out_shape=pltpu.VMEM(queries...  64.3 us

profile of v5, /device:TPU:513, one launch (start us, length us, event | category | flops | bytes accessed | tf_op | source)
XLA Modules:
  0.0 65.1 jit_solution(2675482558916356623)
XLA Ops:
  0.0 64.3 %shard_map.73 = bf16[128,1024]{1,0:T(8,128)(2,1)S(1)} custom-call(bf16[128,1024]{1,0:T(8,128)(2,1)} %q_hbm.1, bf16[128,128]{1,0:T(8,128)(2,1)} %nk_hbm.1, bf16[128,128]{1,0:T(8,128)(2,1)} %nv_hbm.1, bf16[1024,128]{1,0:T(8,128)(2,1)} %ck_hbm.1, bf16[1024,128]{1,0:T(8,128)(2,1)} %cv_hbm.1, s32[16]{0:T(128)} %vl_ref.1, s32[16]{0:T(128)} %bo_ref.1), custom_call_target="tpu_custom_call" | custom-call | tf_op jit(solution)/shard_map/pallas_call | solution.py:341
  64.4 0.7 %copy.9 = bf16[128,1024]{1,0:T(8,128)(2,1)} copy(bf16[128,1024]{1,0:T(8,128)(2,1)S(1)} %shard_map.73) | data formatting | bytes 524288

commit v6 on v5

--- a/solution.py
+++ b/solution.py
@@ -20,8 +20,8 @@
         (3,),
         (17, 9,),
         (7,),
-        (18, 10, 23, 15,),
-        (33, 25,),
+        (18, 10, 23,),
+        (33, 25, 15,),
         (34, 26, 39, 31,),
         (49, 41, 53, 45,),
         (50, 42, 54, 46,),
@@ -34,8 +34,8 @@
         (3,),
         (17, 9,),
         (7,),
-        (18, 10, 23, 15,),
-        (33, 25,),
+        (18, 10, 23,),
+        (33, 25, 15,),
         (34, 26, 39, 31,),
         (49, 41, 53, 45,),
         (50, 42, 54, 46,),

time: 65.2 us -> 64.5 us (0.989)
    pallas_call x1, Pallas kernels: 64.3 us -> 63.7 us  [on_device(): pl.pallas_call(functools.partial(kernel, n), out_shape=pltpu.VMEM(queries...]
where the time goes in v6:
time: 64.5 us; the launch traced here: 64.4 us
  Pallas kernels  63.7 us (99%)
  local copies, waits for them, and re-layouts  0.71 us (1%)
    pallas_call x1, Pallas kernels, on_device(): pl.pallas_call(functools.partial(kernel, n), out_shape=pltpu.VMEM(queries...  63.7 us

profile of v6, /device:TPU:513, one launch (start us, length us, event | category | flops | bytes accessed | tf_op | source)
XLA Modules:
  0.0 64.4 jit_solution(17556074797619442920)
XLA Ops:
  0.0 63.7 %shard_map.73 = bf16[128,1024]{1,0:T(8,128)(2,1)S(1)} custom-call(bf16[128,1024]{1,0:T(8,128)(2,1)} %q_hbm.1, bf16[128,128]{1,0:T(8,128)(2,1)} %nk_hbm.1, bf16[128,128]{1,0:T(8,128)(2,1)} %nv_hbm.1, bf16[1024,128]{1,0:T(8,128)(2,1)} %ck_hbm.1, bf16[1024,128]{1,0:T(8,128)(2,1)} %cv_hbm.1, s32[16]{0:T(128)} %vl_ref.1, s32[16]{0:T(128)} %bo_ref.1), custom_call_target="tpu_custom_call" | custom-call | tf_op jit(solution)/shard_map/pallas_call | solution.py:341
  63.7 0.7 %copy.9 = bf16[128,1024]{1,0:T(8,128)(2,1)} copy(bf16[128,1024]{1,0:T(8,128)(2,1)S(1)} %shard_map.73) | data formatting | bytes 524288
